TPU v7x, 32 devices: a whole 2x2x4 slice. The times are simulated.
32 devices in a mesh: gx: 2 (over core), gy: 4 (over y, x), lev: 4 (over z).
Axes of the slice: x: 2, y: 2, z: 4, core: 2. Of those that a mesh axis runs over, the one named last changes fastest.
Arguments:
- u_wind: float32 [256, 32, 512], P('lev', 'gx', 'gy'), may hold values from -6 to 6
- v_wind: float32 [256, 32, 512], P('lev', 'gx', 'gy'), may hold values from -6 to 6
- w_wind: float32 [256, 32, 512], P('lev', 'gx', 'gy'), may hold values from -4 to 4
- pressure: float32 [256, 32, 512], P('lev', 'gx', 'gy'), may hold values from -6 to 6
- buoyancy: float32 [256, 32, 512], P('lev', 'gx', 'gy'), may hold values from 0.5 to 2
- stiffness: float32 [256, 32, 512], P('lev', 'gx', 'gy'), may hold values from 0.5 to 2
Outputs:
- u_final: float32 [256, 32, 512], P('lev', 'gx', 'gy')
- v_final: float32 [256, 32, 512], P('lev', 'gx', 'gy')
- w_final: float32 [256, 32, 512], P('lev', 'gx', 'gy')
- p_final: float32 [256, 32, 512], P('lev', 'gx', 'gy')
All inputs are finite; a program needn't handle non-finite values.
Results may differ from a plain program's by a relative error of at most 0.002.
Values sent between devices are 32-bit elements; how exact they have to be, the bound alone decides.
A program may use at most 128 MiB of HBM per device.

v0:
```python
import jax
import jax.numpy as jnp
from jax import lax
from jax.sharding import PartitionSpec as P

SUBSTEPS = 3


courant_h = 0.3
vertical_gain = 4096.0


def shifted(block, axis, distance):
    devices = range(lax.axis_size(axis))
    route = [(i - distance, i) for i in devices if i - distance in devices]
    return lax.ppermute(block, axis, route)


def with_halo(x, sides, width):
    for axis, dim in sides:
        count, length = (lax.axis_size(axis), x.shape[dim])
        up = [(i, (i + 1) % count) for i in range(count)]
        down = [(j, i) for i, j in up]
        last = lax.slice_in_dim(x, length - width, length, axis=dim)
        initial = lax.slice_in_dim(x, 0, width, axis=dim)
        before = lax.ppermute(last, axis, up)
        after = lax.ppermute(initial, axis, down)
        x = jnp.concatenate([before, x, after], axis=dim)
    return x


def rows_below(grid_field, stride, fill_value):
    padding = jnp.full((stride,) + grid_field.shape[1:], fill_value, grid_field.dtype)
    return jnp.concatenate([padding, grid_field[:-stride]], 0)


def rows_above(grid_field, stride, fill_value):
    padding = jnp.full((stride,) + grid_field.shape[1:], fill_value, grid_field.dtype)
    return jnp.concatenate([grid_field[stride:], padding], 0)


def eliminate(own_rows, from_below, from_above):
    factor_low = own_rows[0] / from_below[1]
    factor_high = own_rows[2] / from_above[1]
    new_lower = -factor_low * from_below[0]
    new_upper = -factor_high * from_above[2]
    new_main = own_rows[1] - factor_low * from_below[2] - factor_high * from_above[0]
    side_terms = tuple(
        (
            own_rows[member] - factor_low * from_below[member] - factor_high * from_above[member]
            for member in range(3, len(own_rows))
        )
    )
    return (new_lower, new_main, new_upper) + side_terms


def local_solve(lower_band, main_band, upper_band, right_sides):
    row_count = main_band.shape[0]
    bands = (lower_band, main_band, upper_band) + tuple(right_sides)
    fill_values = (0.0, 1.0) + (0.0,) * (len(bands) - 2)
    stride = 1
    while stride < row_count:
        below_rows = tuple(
            (
                rows_below(member, stride, fill_value)
                for member, fill_value in zip(bands, fill_values)
            )
        )
        above_rows = tuple(
            (
                rows_above(member, stride, fill_value)
                for member, fill_value in zip(bands, fill_values)
            )
        )
        bands = eliminate(bands, below_rows, above_rows)
        stride = stride * 2
    return tuple((member / bands[1] for member in bands[3:]))


def shards(u_wind, v_wind, w_wind, pressure, buoyancy, stiffness):
    level_count = pressure.shape[0]
    position = lax.axis_index("lev")
    groups = lax.axis_size("lev")
    level_index = lax.broadcasted_iota(jnp.int32, pressure.shape, 0)
    is_last = level_index == level_count - 1
    stiff_next = shifted(stiffness[0], "lev", -1)
    stiff_up = jnp.concatenate([stiffness[1:], stiff_next[None]], 0)
    lower_band = -vertical_gain * buoyancy * stiffness
    upper_band = -vertical_gain * buoyancy * stiff_up
    main_band = 1.0 + vertical_gain * buoyancy * (stiffness + stiff_up)
    inner_lower = jnp.where((level_index == 0) | is_last, 0.0, lower_band)
    inner_upper = jnp.where(level_index >= level_count - 2, 0.0, upper_band)
    inner_main = jnp.where(is_last, 1.0, main_band)
    bottom_link = jnp.where((level_index == 0) & (position > 0), lower_band, 0.0)
    top_link = jnp.where(level_index == level_count - 2, upper_band, 0.0)
    for substep in range(SUBSTEPS):
        p_edge = with_halo(pressure, (("gx", 1), ("gy", 2)), 1)
        u_new = u_wind - courant_h * buoyancy * (p_edge[:, 2:, 1:-1] - p_edge[:, :-2, 1:-1])
        v_new = v_wind - courant_h * buoyancy * (p_edge[:, 1:-1, 2:] - p_edge[:, 1:-1, :-2])
        moment_edge = with_halo(jnp.stack([u_new, v_new]), (("gx", 2), ("gy", 3)), 1)
        divergence = (
            moment_edge[0, :, 2:, 1:-1]
            - moment_edge[0, :, :-2, 1:-1]
            + (moment_edge[1, :, 1:-1, 2:] - moment_edge[1, :, 1:-1, :-2])
        )
        p_star = pressure - courant_h * stiffness * divergence
        p_next = shifted(p_star[0], "lev", -1)
        p_above = jnp.concatenate([p_star[1:], p_next[None]], 0)
        right_side = w_wind - vertical_gain * buoyancy * (p_above - p_star)
        inner_side = jnp.where(is_last, 0.0, right_side)
        solved, low_part, high_part = local_solve(
            inner_lower, inner_main, inner_upper, (inner_side, bottom_link, top_link)
        )
        first_rows = jnp.stack([solved[0], low_part[0], high_part[0]])
        next_rows = shifted(first_rows, "lev", -1)
        last_lower = lower_band[-1]
        last_upper = upper_band[-1]
        alpha_row = -last_lower * low_part[-2]
        beta_row = main_band[-1] - last_lower * high_part[-2] - last_upper * next_rows[1]
        gamma_row = -last_upper * next_rows[2]
        rho_row = right_side[-1] - last_lower * solved[-2] - last_upper * next_rows[0]
        reduced = lax.all_gather(
            jnp.stack([alpha_row, beta_row, gamma_row, rho_row])[None], "lev", axis=0, tiled=True
        )
        ratio_rows = [reduced[0, 2] / reduced[0, 1]]
        value_rows = [reduced[0, 3] / reduced[0, 1]]
        for member in range(1, groups):
            pivot_row = reduced[member, 1] - reduced[member, 0] * ratio_rows[-1]
            ratio_rows.append(reduced[member, 2] / pivot_row)
            value_rows.append(
                (reduced[member, 3] - reduced[member, 0] * value_rows[-1]) / pivot_row
            )
        solution = [value_rows[-1]]
        for member in range(groups - 2, -1, -1):
            solution.insert(0, value_rows[member] - ratio_rows[member] * solution[0])
        padded = jnp.stack([jnp.zeros_like(rho_row)] + solution)
        prev_top = lax.dynamic_index_in_dim(padded, position, 0, keepdims=False)
        own_top = lax.dynamic_index_in_dim(padded, position + 1, 0, keepdims=False)
        w_new = jnp.where(is_last, own_top, solved - low_part * prev_top - high_part * own_top)
        w_below = jnp.concatenate([prev_top[None], w_new[:-1]], 0)
        pressure = p_star - stiffness * (w_new - w_below)
        u_wind, v_wind, w_wind = (u_new, v_new, w_new)
    return (u_wind, v_wind, w_wind, pressure)


def solution(mesh):
    return jax.shard_map(
        shards,
        mesh=mesh,
        in_specs=(
            P("lev", "gx", "gy"),
            P("lev", "gx", "gy"),
            P("lev", "gx", "gy"),
            P("lev", "gx", "gy"),
            P("lev", "gx", "gy"),
            P("lev", "gx", "gy"),
        ),
        out_specs=(
            P("lev", "gx", "gy"),
            P("lev", "gx", "gy"),
            P("lev", "gx", "gy"),
            P("lev", "gx", "gy"),
        ),
        check_vma=False,
    )
```

profile of v0, /device:TPU:0, one launch (start us, length us, event | category | flops | bytes accessed | tf_op | source)
XLA Modules:
  0.0 220.8 jit_solution(3149249265771003646)
XLA Ops:
  0.6 1.1 fusion.174
  3.0 1.3 collective-permute-start.8
  4.4 1.2 pad_maximum_fusion.3
  6.1 3.9 %collective-permute-start.2 = (f32[64,18,1]{0,2,1:T(1,128)S(1)}, f32[64,18,1]{0,2,1:T(1,128)S(1)}, u32[]{:S(2)}, u32[]{:S(2)}) collective-permute-start(f32[64,18,1]{0,2,1:T(1,128)S(1)} %copy.88), channel_id=1, source_target_pairs={{4,0},{8,4},{12,8},{0,12},{5,1},{9,5},{13,9},{1,13},{6,2},{10,6},{... | collective-permute-start | bytes 13832 | tf_op jit(solution)/shard_map/ppermute | solution.py:27
  10.3 1.1 collective-permute-done.2
  11.7 3.1 %collective-permute-done.3 = f32[64,18,1]{0,2,1:T(1,128)S(1)} collective-permute-done((f32[64,18,1]{0,2,1:T(1,128)S(1)}, f32[64,18,1]{0,2,1:T(1,128)S(1)}, u32[]{:S(2)}, u32[]{:S(2)}) %collective-permute-start.3) | collective-permute-done | bytes 4640 | tf_op jit(solution)/shard_map/ppermute | solution.py:26
  15.2 1.9 fusion.103
  18.9 2.2 fusion.122
  21.1 1.9 copy.92
  23.7 2.0 collective-permute-start.7
  25.7 1.3 collective-permute-done.6
  27.0 1.7 copy.93
  28.7 1.7 copy.95
  30.4 2.0 fusion.28
  32.4 1.6 collective-permute-start.9
  34.2 4.6 %collective-permute-done.9 = f32[16,128]{1,0:T(8,128)S(1)} collective-permute-done((f32[16,128]{1,0:T(8,128)S(1)}, f32[16,128]{1,0:T(8,128)S(1)}, u32[]{:S(2)}, u32[]{:S(2)}) %collective-permute-start.9) | collective-permute-done | bytes 8224 | tf_op jit(solution)/shard_map/ppermute | solution.py:16
  38.7 1.3 broadcast_select_fusion.3
  51.1 1.3 collective-permute-start.10
  53.0 3.8 %collective-permute-done.10 = f32[3,16,128]{2,1,0:T(8,128)S(1)} collective-permute-done((f32[3,16,128]{2,1,0:T(8,128)S(1)}, f32[3,16,128]{2,1,0:T(8,128)S(1)}, u32[]{:S(2)}, u32[]{:S(2)}) %collective-permute-start.10) | collective-permute-done | bytes 24608 | tf_op jit(solution)/shard_map/ppermute | solution.py:16
  56.8 1.4 fusion.101
  58.2 14.0 %all-gather = f32[16,16,128]{2,1,0:T(8,128)S(1)} all-gather(f32[4,16,128]{2,1,0:T(8,128)S(1)} %fusion.49), channel_id=2, replica_groups=mesh['gx'=2,'gy'=4,'lev'=4] {'lev'}, dimensions={0}, use_global_device_ids=true | all-gather | bytes 163840 | tf_op jit(solution)/shard_map/all_gather | solution.py:122
  75.4 1.5 subtract_select_fusion.2
  79.4 1.4 fusion.124
  80.8 2.0 copy.96
  83.7 2.0 copy.98
  85.6 1.1 collective-permute-start.14
  86.7 1.9 copy.97
  88.7 1.8 collective-permute-done.14
  90.5 1.9 copy.99
  92.4 3.5 %fusion.20 = (f32[64,16,128]{2,1,0:T(8,128)S(1)}, f32[64,16,128]{2,1,0:T(8,128)S(1)}) fusion(f32[64,16,128]{2,1,0:T(8,128)} %copy-done.5, f32[64,18,1]{2,1,0:T(8,128)} %copy.99, f32[64,1,128]{2,1,0:T(1,128)S(1)} %collective-permute-done.11, f32[64,16,128]{2,1,0:T(8,128)} %copy-done.29, f32[64,1,128]{2,1,0:T(1,128)S(1)} %collective-permute-done.12, ...), kind=kLoop, calls=%fused_computation.59 | loop fusion | flops 2621440 | bytes 3810304 | tf_op jit(solution)/shard_map/sub | solution.py:99
  97.8 2.2 fusion.121
  100.0 2.4 %copy.100 = f32[2,64,18,1]{1,0,3,2:T(2,128)} copy(f32[2,64,18,1]{3,2,1,0:T(8,128)} %get-tuple-element.71) | data formatting | bytes 18432 | tf_op jit(solution)/shard_map/slice | solution.py:25
  102.5 2.4 %copy.102 = f32[2,64,18,1]{1,0,3,2:T(2,128)} copy(f32[2,64,18,1]{3,2,1,0:T(8,128)} %get-tuple-element.72) | data formatting | bytes 18432 | tf_op jit(solution)/shard_map/slice | solution.py:24
  104.9 1.9 collective-permute-start.18
  106.8 2.4 %copy.101 = f32[2,64,18,1]{3,2,1,0:T(8,128)} copy(f32[2,64,18,1]{1,0,3,2:T(2,128)} %collective-permute-done.17) | data formatting | bytes 18432 | tf_op jit(solution)/shard_map/ppermute | solution.py:27
  109.9 2.4 %copy.103 = f32[2,64,18,1]{3,2,1,0:T(8,128)} copy(f32[2,64,18,1]{1,0,3,2:T(2,128)} %collective-permute-done.18) | data formatting | bytes 18432 | tf_op jit(solution)/shard_map/ppermute | solution.py:26
  112.3 2.8 %fusion.16 = f32[64,16,128]{2,1,0:T(8,128)S(1)} fusion(f32[64,16,128]{2,1,0:T(8,128)} %copy-done.29, f32[2,64,18,1]{3,2,1,0:T(8,128)} %copy.103, f32[2,64,1,128]{3,2,1,0:T(1,128)S(1)} %collective-permute-done.15, f32[2,64,1,128]{3,2,1,0:T(1,128)S(1)} %collective-permute-done.16, f32[1,64,16,128]{3,2,1,0:T(8,128)} %bitcast.330, ...), kind=kLoop, calls=%fused_computation.43 | loop fusion | flops 2359296 | bytes 2770944 | tf_op jit(solution)/shard_map/sub | solution.py:106
  115.2 1.3 collective-permute-start.19
  116.5 4.2 %collective-permute-done.19 = f32[16,128]{1,0:T(8,128)S(1)} collective-permute-done((f32[16,128]{1,0:T(8,128)S(1)}, f32[16,128]{1,0:T(8,128)S(1)}, u32[]{:S(2)}, u32[]{:S(2)}) %collective-permute-start.19) | collective-permute-done | bytes 8224 | tf_op jit(solution)/shard_map/ppermute | solution.py:16
  122.4 0.9 copy-done.3
  128.8 1.3 collective-permute-start.20
  130.1 4.4 %collective-permute-done.20 = f32[3,16,128]{2,1,0:T(8,128)S(1)} collective-permute-done((f32[3,16,128]{2,1,0:T(8,128)S(1)}, f32[3,16,128]{2,1,0:T(8,128)S(1)}, u32[]{:S(2)}, u32[]{:S(2)}) %collective-permute-start.20) | collective-permute-done | bytes 24608 | tf_op jit(solution)/shard_map/ppermute | solution.py:16
  135.2 13.4 %all-gather.1 = f32[16,16,128]{2,1,0:T(8,128)S(1)} all-gather(f32[4,16,128]{2,1,0:T(8,128)S(1)} %fusion.51), channel_id=3, replica_groups=mesh['gx'=2,'gy'=4,'lev'=4] {'lev'}, dimensions={0}, use_global_device_ids=true | all-gather | bytes 163840 | tf_op jit(solution)/shard_map/all_gather | solution.py:122
  151.3 1.4 fusion.123
  152.7 1.4 copy.104
  154.2 1.8 collective-permute-start.23
  155.9 1.4 copy.106
  157.9 1.2 copy.105
  159.1 2.9 %collective-permute-done.24 = f32[64,18,1]{0,1,2:T(8,128)S(1)} collective-permute-done((f32[64,18,1]{0,1,2:T(8,128)S(1)}, f32[64,18,1]{0,1,2:T(8,128)S(1)}, u32[]{:S(2)}, u32[]{:S(2)}) %collective-permute-start.24) | collective-permute-done | bytes 4640 | tf_op jit(solution)/shard_map/ppermute | solution.py:26
  162.0 1.2 copy.107
  163.2 3.2 %fusion.8 = (f32[64,16,128]{2,1,0:T(8,128)S(1)}, f32[64,16,128]{2,1,0:T(8,128)S(1)}) fusion(f32[64,16,128]{2,1,0:T(8,128)} %copy-done.6, f32[64,18,1]{2,1,0:T(8,128)} %copy.107, f32[64,1,128]{2,1,0:T(1,128)S(1)} %collective-permute-done.21, f32[64,16,128]{2,1,0:T(8,128)} %copy-done.26, f32[64,1,128]{2,1,0:T(1,128)S(1)} %collective-permute-done.22, ...), kind=kLoop, calls=%fused_computation.27 | loop fusion | flops 1966080 | bytes 3220480 | tf_op jit(solution)/shard_map/sub | solution.py:99
  168.3 2.2 fusion.120
  170.5 2.4 %copy.108 = f32[2,64,18,1]{1,0,3,2:T(2,128)} copy(f32[2,64,18,1]{3,2,1,0:T(8,128)} %get-tuple-element.69) | data formatting | bytes 18432 | tf_op jit(solution)/shard_map/slice | solution.py:25
  173.3 2.4 %copy.110 = f32[2,64,18,1]{1,0,3,2:T(2,128)} copy(f32[2,64,18,1]{3,2,1,0:T(8,128)} %get-tuple-element.70) | data formatting | bytes 18432 | tf_op jit(solution)/shard_map/slice | solution.py:24
  175.8 1.6 collective-permute-start.28
  177.4 2.4 %copy.109 = f32[2,64,18,1]{3,2,1,0:T(8,128)} copy(f32[2,64,18,1]{1,0,3,2:T(2,128)} %collective-permute-done.27) | data formatting | bytes 18432 | tf_op jit(solution)/shard_map/ppermute | solution.py:27
  180.7 2.4 %copy.111 = f32[2,64,18,1]{3,2,1,0:T(8,128)} copy(f32[2,64,18,1]{1,0,3,2:T(2,128)} %collective-permute-done.28) | data formatting | bytes 18432 | tf_op jit(solution)/shard_map/ppermute | solution.py:26
  183.2 2.8 %fusion.4 = f32[64,16,128]{2,1,0:T(8,128)S(1)} fusion(f32[64,16,128]{2,1,0:T(8,128)} %copy-done.26, f32[2,64,18,1]{3,2,1,0:T(8,128)} %copy.111, f32[2,64,1,128]{3,2,1,0:T(1,128)S(1)} %collective-permute-done.25, f32[2,64,1,128]{3,2,1,0:T(1,128)S(1)} %collective-permute-done.26, f32[1,64,16,128]{3,2,1,0:T(8,128)} %bitcast.336, ...), kind=kLoop, calls=%fused_computation.11 | loop fusion | flops 2359296 | bytes 2770944 | tf_op jit(solution)/shard_map/sub | solution.py:106
  186.0 1.3 collective-permute-start.29
  187.4 4.2 %collective-permute-done.29 = f32[16,128]{1,0:T(8,128)S(1)} collective-permute-done((f32[16,128]{1,0:T(8,128)S(1)}, f32[16,128]{1,0:T(8,128)S(1)}, u32[]{:S(2)}, u32[]{:S(2)}) %collective-permute-start.29) | collective-permute-done | bytes 8224 | tf_op jit(solution)/shard_map/ppermute | solution.py:16
  199.6 1.3 collective-permute-start.30
  200.9 4.4 %collective-permute-done.30 = f32[3,16,128]{2,1,0:T(8,128)S(1)} collective-permute-done((f32[3,16,128]{2,1,0:T(8,128)S(1)}, f32[3,16,128]{2,1,0:T(8,128)S(1)}, u32[]{:S(2)}, u32[]{:S(2)}) %collective-permute-start.30) | collective-permute-done | bytes 24608 | tf_op jit(solution)/shard_map/ppermute | solution.py:16
  206.1 13.4 %all-gather.2 = f32[16,16,128]{2,1,0:T(8,128)S(1)} all-gather(f32[4,16,128]{2,1,0:T(8,128)S(1)} %fusion.53), channel_id=4, replica_groups=mesh['gx'=2,'gy'=4,'lev'=4] {'lev'}, dimensions={0}, use_global_device_ids=true | all-gather | bytes 163840 | tf_op jit(solution)/shard_map/all_gather | solution.py:122
  219.8 1.0 fusion.47
  (330 shorter events, 48.8 us)
Async XLA Ops:
  1.7 2.6 %collective-permute-start = (f32[64,1,128]{2,1,0:T(1,128)S(1)}, f32[64,1,128]{2,1,0:T(1,128)S(1)}, u32[]{:S(2)}, u32[]{:S(2)}) collective-permute-start(f32[64,1,128]{2,1,0:T(1,128)S(1)} %get-tuple-element.238), channel_id=1, source_target_pairs={{16,0},{0,16},{17,1},{1,17},{18,2},{2,18},{19,3},{3,19},{20,4},{4,... | collective-permute-start | bytes 98312 | tf_op jit(solution)/shard_map/ppermute | solution.py:27
  2.3 2.1 collective-permute-start.1
  3.0 31.1 %collective-permute-start.8 = (f32[16,128]{1,0:T(8,128)S(1)}, f32[16,128]{1,0:T(8,128)S(1)}, u32[]{:S(2)}, u32[]{:S(2)}) collective-permute-start(f32[16,128]{1,0:T(8,128)S(1)} %slice_bitcast_fusion.36), channel_id=1, source_target_pairs={{1,0},{2,1},{3,2},{5,4},{6,5},{7,6},{9,8},{10,9},{11,10},{13,12},{... | collective-permute-start | bytes 24584 | tf_op jit(solution)/shard_map/ppermute | solution.py:16
  5.8 9.4 %copy-start.1 = (f32[64,16,128]{2,1,0:T(8,128)S(1)}, f32[64,16,128]{2,1,0:T(8,128)}, u32[]{:S(2)}) copy-start(f32[64,16,128]{2,1,0:T(8,128)} %param.10) | copy-start | bytes 1572868
  5.8 9.4 %copy-start.27 = (f32[64,16,128]{2,1,0:T(8,128)S(1)}, f32[64,16,128]{2,1,0:T(8,128)}, u32[]{:S(2)}) copy-start(f32[64,16,128]{2,1,0:T(8,128)} %param.9) | copy-start | bytes 1572868
  6.1 5.3 %collective-permute-start.2 = (f32[64,18,1]{0,2,1:T(1,128)S(1)}, f32[64,18,1]{0,2,1:T(1,128)S(1)}, u32[]{:S(2)}, u32[]{:S(2)}) collective-permute-start(f32[64,18,1]{0,2,1:T(1,128)S(1)} %copy.88), channel_id=1, source_target_pairs={{4,0},{8,4},{12,8},{0,12},{5,1},{9,5},{13,9},{1,13},{6,2},{10,6},{... | collective-permute-start | bytes 13832 | tf_op jit(solution)/shard_map/ppermute | solution.py:27
  10.2 4.6 %collective-permute-start.3 = (f32[64,18,1]{0,2,1:T(1,128)S(1)}, f32[64,18,1]{0,2,1:T(1,128)S(1)}, u32[]{:S(2)}, u32[]{:S(2)}) collective-permute-start(f32[64,18,1]{0,2,1:T(1,128)S(1)} %copy.90), channel_id=1, source_target_pairs={{0,4},{4,8},{8,12},{12,0},{1,5},{5,9},{9,13},{13,1},{2,6},{6,10},{... | collective-permute-start | bytes 13832 | tf_op jit(solution)/shard_map/ppermute | solution.py:26
  17.0 1.9 copy-start.38
  17.0 13.4 %copy-start.5 = (f32[64,16,128]{2,1,0:T(8,128)}, f32[64,16,128]{2,1,0:T(8,128)S(1)}, u32[]{:S(2)}) copy-start(f32[64,16,128]{2,1,0:T(8,128)S(1)} %get-tuple-element.80) | copy-start | bytes 1572868
  17.2 1.3 collective-permute-start.4
  17.2 1.4 collective-permute-start.5
  17.7 57.7 %copy-start.72 = (pred[64]{0:T(512)(128)(4,1)}, pred[64]{0:T(512)(128)(4,1)S(1)}, u32[]{:S(2)}) copy-start(pred[64]{0:T(512)(128)(4,1)S(1)} %iota_compare_fusion.2) | copy-start | bytes 196
  21.1 2.1 copy-start.61
  23.1 3.9 %collective-permute-start.6 = (f32[2,64,18,1]{1,0,3,2:T(2,128)S(1)}, f32[2,64,18,1]{1,0,3,2:T(2,128)S(1)}, u32[]{:S(2)}, u32[]{:S(2)}) collective-permute-start(f32[2,64,18,1]{1,0,3,2:T(2,128)S(1)} %copy.92), channel_id=1, source_target_pairs={{4,0},{8,4},{12,8},{0,12},{5,1},{9,5},{13,9},{1,13},{6,2},{10,6},{... | collective-permute-start | bytes 27656 | tf_op jit(solution)/shard_map/ppermute | solution.py:27
  23.7 5.0 %collective-permute-start.7 = (f32[2,64,18,1]{1,0,3,2:T(2,128)S(1)}, f32[2,64,18,1]{1,0,3,2:T(2,128)S(1)}, u32[]{:S(2)}, u32[]{:S(2)}) collective-permute-start(f32[2,64,18,1]{1,0,3,2:T(2,128)S(1)} %copy.94), channel_id=1, source_target_pairs={{0,4},{4,8},{8,12},{12,0},{1,5},{5,9},{9,13},{13,1},{2,6},{6,10},{... | collective-permute-start | bytes 27656 | tf_op jit(solution)/shard_map/ppermute | solution.py:26
  25.6 4.8 %copy-start = (f32[64,16,128]{2,1,0:T(8,128)S(1)}, f32[64,16,128]{2,1,0:T(8,128)}, u32[]{:S(2)}) copy-start(f32[64,16,128]{2,1,0:T(8,128)} %param.11) | copy-start | bytes 1572868
  25.6 4.8 %copy-start.28 = (f32[64,16,128]{2,1,0:T(8,128)S(1)}, f32[64,16,128]{2,1,0:T(8,128)}, u32[]{:S(2)}) copy-start(f32[64,16,128]{2,1,0:T(8,128)} %param.9) | copy-start | bytes 1572868
  25.6 4.8 %copy-start.39 = (f32[1,64,16,128]{3,2,1,0:T(8,128)S(1)}, f32[1,64,16,128]{3,2,1,0:T(8,128)}, u32[]{:S(2)}) copy-start(f32[1,64,16,128]{3,2,1,0:T(8,128)} %copy-done.38) | copy-start | bytes 1572868
  32.4 7.6 %copy-start.40 = (f32[64,16,128]{2,1,0:T(8,128)}, f32[64,16,128]{2,1,0:T(8,128)S(1)}, u32[]{:S(2)}) copy-start(f32[64,16,128]{2,1,0:T(8,128)S(1)} %fusion.28) | copy-start | bytes 1572868
  32.4 6.3 %copy-start.66 = (f32[64,16,128]{2,1,0:T(8,128)S(1)}, f32[64,16,128]{2,1,0:T(8,128)}, u32[]{:S(2)}) copy-start(f32[64,16,128]{2,1,0:T(8,128)} %param.8) | copy-start | bytes 1572868
  32.4 6.3 %collective-permute-start.9 = (f32[16,128]{1,0:T(8,128)S(1)}, f32[16,128]{1,0:T(8,128)S(1)}, u32[]{:S(2)}, u32[]{:S(2)}) collective-permute-start(f32[16,128]{1,0:T(8,128)S(1)} %slice_bitcast_fusion.35), channel_id=1, source_target_pairs={{1,0},{2,1},{3,2},{5,4},{6,5},{7,6},{9,8},{10,9},{11,10},{13,12},{... | collective-permute-start | bytes 24584 | tf_op jit(solution)/shard_map/ppermute | solution.py:16
  51.1 5.7 %collective-permute-start.10 = (f32[3,16,128]{2,1,0:T(8,128)S(1)}, f32[3,16,128]{2,1,0:T(8,128)S(1)}, u32[]{:S(2)}, u32[]{:S(2)}) collective-permute-start(f32[3,16,128]{2,1,0:T(8,128)S(1)} %pad_maximum_fusion.78), channel_id=1, source_target_pairs={{1,0},{2,1},{3,2},{5,4},{6,5},{7,6},{9,8},{10,9},{11,10},{13,12},{... | collective-permute-start | bytes 73736 | tf_op jit(solution)/shard_map/ppermute | solution.py:16
  58.2 18.8 %copy-start.67 = (f32[1,16,128]{2,1,0:T(8,128)}, f32[1,16,128]{2,1,0:T(8,128)S(1)}, u32[]{:S(2)}) copy-start(f32[1,16,128]{2,1,0:T(8,128)S(1)} %get-tuple-element.166) | copy-start | bytes 24580
  75.4 1.6 copy-start.41
  77.8 3.0 %copy-start.29 = (f32[64,16,128]{2,1,0:T(8,128)}, f32[64,16,128]{2,1,0:T(8,128)S(1)}, u32[]{:S(2)}) copy-start(f32[64,16,128]{2,1,0:T(8,128)S(1)} %fusion.39) | copy-start | bytes 1572868
  77.8 1.3 collective-permute-start.11
  77.9 1.4 collective-permute-start.12
  82.7 4.0 %collective-permute-start.13 = (f32[64,18,1]{0,2,1:T(1,128)}, f32[64,18,1]{0,2,1:T(1,128)}, u32[]{:S(2)}, u32[]{:S(2)}) collective-permute-start(f32[64,18,1]{0,2,1:T(1,128)} %copy.96), channel_id=1, source_target_pairs={{4,0},{8,4},{12,8},{0,12},{5,1},{9,5},{13,9},{1,13},{6,2},{10,6},{... | collective-permute-start | bytes 13832 | tf_op jit(solution)/shard_map/ppermute | solution.py:27
  85.6 4.9 %collective-permute-start.14 = (f32[64,18,1]{0,2,1:T(1,128)}, f32[64,18,1]{0,2,1:T(1,128)}, u32[]{:S(2)}, u32[]{:S(2)}) collective-permute-start(f32[64,18,1]{0,2,1:T(1,128)} %copy.98), channel_id=1, source_target_pairs={{0,4},{4,8},{8,12},{12,0},{1,5},{5,9},{9,13},{13,1},{2,6},{6,10},{... | collective-permute-start | bytes 13832 | tf_op jit(solution)/shard_map/ppermute | solution.py:26
  95.9 1.8 copy-start.6
  95.9 1.8 copy-start.7
  96.0 1.3 collective-permute-start.15
  96.1 1.4 collective-permute-start.16
  102.4 4.4 %collective-permute-start.17 = (f32[2,64,18,1]{1,0,3,2:T(2,128)}, f32[2,64,18,1]{1,0,3,2:T(2,128)}, u32[]{:S(2)}, u32[]{:S(2)}) collective-permute-start(f32[2,64,18,1]{1,0,3,2:T(2,128)} %copy.100), channel_id=1, source_target_pairs={{4,0},{8,4},{12,8},{0,12},{5,1},{9,5},{13,9},{1,13},{6,2},{10,6},{... | collective-permute-start | bytes 27656 | tf_op jit(solution)/shard_map/ppermute | solution.py:27
  104.9 5.0 %collective-permute-start.18 = (f32[2,64,18,1]{1,0,3,2:T(2,128)}, f32[2,64,18,1]{1,0,3,2:T(2,128)}, u32[]{:S(2)}, u32[]{:S(2)}) collective-permute-start(f32[2,64,18,1]{1,0,3,2:T(2,128)} %copy.102), channel_id=1, source_target_pairs={{0,4},{4,8},{8,12},{12,0},{1,5},{5,9},{9,13},{13,1},{2,6},{6,10},{... | collective-permute-start | bytes 27656 | tf_op jit(solution)/shard_map/ppermute | solution.py:26
  112.3 8.4 %copy-start.49 = (f32[64,16,128]{2,1,0:T(8,128)S(1)}, f32[64,16,128]{2,1,0:T(8,128)}, u32[]{:S(2)}) copy-start(f32[64,16,128]{2,1,0:T(8,128)} %copy-done.48) | copy-start | bytes 1572868
  112.3 8.4 %copy-start.73 = (pred[64]{0:T(512)(128)(4,1)S(1)}, pred[64]{0:T(512)(128)(4,1)}, u32[]{:S(2)}) copy-start(pred[64]{0:T(512)(128)(4,1)} %copy-done.72) | copy-start | bytes 196
  115.2 5.5 %collective-permute-start.19 = (f32[16,128]{1,0:T(8,128)S(1)}, f32[16,128]{1,0:T(8,128)S(1)}, u32[]{:S(2)}, u32[]{:S(2)}) collective-permute-start(f32[16,128]{1,0:T(8,128)S(1)} %slice_bitcast_fusion.23), channel_id=1, source_target_pairs={{1,0},{2,1},{3,2},{5,4},{6,5},{7,6},{9,8},{10,9},{11,10},{13,12},{... | collective-permute-start | bytes 24584 | tf_op jit(solution)/shard_map/ppermute | solution.py:16
  126.1 1.2 copy-start.46
  128.4 6.1 %copy-start.70 = (f32[1,16,128]{2,1,0:T(8,128)S(1)}, f32[1,16,128]{2,1,0:T(8,128)}, u32[]{:S(2)}) copy-start(f32[1,16,128]{2,1,0:T(8,128)} %get-tuple-element.34) | copy-start | bytes 24580
  128.4 6.8 %copy-start.68 = (f32[1,16,128]{2,1,0:T(8,128)S(1)}, f32[1,16,128]{2,1,0:T(8,128)}, u32[]{:S(2)}) copy-start(f32[1,16,128]{2,1,0:T(8,128)} %copy-done.67) | copy-start | bytes 24580
  128.4 20.3 %copy-start.31 = (f32[64,16,128]{2,1,0:T(8,128)S(1)}, f32[64,16,128]{2,1,0:T(8,128)}, u32[]{:S(2)}) copy-start(f32[64,16,128]{2,1,0:T(8,128)} %copy-done.30) | copy-start | bytes 1572868
  128.4 20.3 %copy-start.34 = (f32[64,16,128]{2,1,0:T(8,128)S(1)}, f32[64,16,128]{2,1,0:T(8,128)}, u32[]{:S(2)}) copy-start(f32[64,16,128]{2,1,0:T(8,128)} %copy-done.33) | copy-start | bytes 1572868
  128.8 5.7 %collective-permute-start.20 = (f32[3,16,128]{2,1,0:T(8,128)S(1)}, f32[3,16,128]{2,1,0:T(8,128)S(1)}, u32[]{:S(2)}, u32[]{:S(2)}) collective-permute-start(f32[3,16,128]{2,1,0:T(8,128)S(1)} %pad_maximum_fusion.77), channel_id=1, source_target_pairs={{1,0},{2,1},{3,2},{5,4},{6,5},{7,6},{9,8},{10,9},{11,10},{13,12},{... | collective-permute-start | bytes 73736 | tf_op jit(solution)/shard_map/ppermute | solution.py:16
  149.7 3.0 %copy-start.26 = (f32[64,16,128]{2,1,0:T(8,128)}, f32[64,16,128]{2,1,0:T(8,128)S(1)}, u32[]{:S(2)}) copy-start(f32[64,16,128]{2,1,0:T(8,128)S(1)} %fusion.43) | copy-start | bytes 1572868
  149.8 1.3 collective-permute-start.21
  149.9 1.4 collective-permute-start.22
  154.2 3.7 %collective-permute-start.23 = (f32[64,18,1]{0,1,2:T(8,128)S(1)}, f32[64,18,1]{0,1,2:T(8,128)S(1)}, u32[]{:S(2)}, u32[]{:S(2)}) collective-permute-start(f32[64,18,1]{0,1,2:T(8,128)S(1)} %copy.104), channel_id=1, source_target_pairs={{4,0},{8,4},{12,8},{0,12},{5,1},{9,5},{13,9},{1,13},{6,2},{10,6},{... | collective-permute-start | bytes 13832 | tf_op jit(solution)/shard_map/ppermute | solution.py:27
  157.3 4.6 %collective-permute-start.24 = (f32[64,18,1]{0,1,2:T(8,128)S(1)}, f32[64,18,1]{0,1,2:T(8,128)S(1)}, u32[]{:S(2)}, u32[]{:S(2)}) collective-permute-start(f32[64,18,1]{0,1,2:T(8,128)S(1)} %copy.106), channel_id=1, source_target_pairs={{0,4},{4,8},{8,12},{12,0},{1,5},{5,9},{9,13},{13,1},{2,6},{6,10},{... | collective-permute-start | bytes 13832 | tf_op jit(solution)/shard_map/ppermute | solution.py:26
  166.4 1.9 copy-start.36
  166.4 1.9 copy-start.37
  166.5 1.3 collective-permute-start.25
  166.6 1.4 collective-permute-start.26
  172.9 4.4 %collective-permute-start.27 = (f32[2,64,18,1]{1,0,3,2:T(2,128)}, f32[2,64,18,1]{1,0,3,2:T(2,128)}, u32[]{:S(2)}, u32[]{:S(2)}) collective-permute-start(f32[2,64,18,1]{1,0,3,2:T(2,128)} %copy.108), channel_id=1, source_target_pairs={{4,0},{8,4},{12,8},{0,12},{5,1},{9,5},{13,9},{1,13},{6,2},{10,6},{... | collective-permute-start | bytes 27656 | tf_op jit(solution)/shard_map/ppermute | solution.py:27
  175.8 5.0 %collective-permute-start.28 = (f32[2,64,18,1]{1,0,3,2:T(2,128)}, f32[2,64,18,1]{1,0,3,2:T(2,128)}, u32[]{:S(2)}, u32[]{:S(2)}) collective-permute-start(f32[2,64,18,1]{1,0,3,2:T(2,128)} %copy.110), channel_id=1, source_target_pairs={{0,4},{4,8},{8,12},{12,0},{1,5},{5,9},{9,13},{13,1},{2,6},{6,10},{... | collective-permute-start | bytes 27656 | tf_op jit(solution)/shard_map/ppermute | solution.py:26
  183.2 8.4 %copy-start.51 = (f32[64,16,128]{2,1,0:T(8,128)S(1)}, f32[64,16,128]{2,1,0:T(8,128)}, u32[]{:S(2)}) copy-start(f32[64,16,128]{2,1,0:T(8,128)} %copy-done.50) | copy-start | bytes 1572868
  183.2 8.4 %copy-start.74 = (pred[64]{0:T(512)(128)(4,1)S(1)}, pred[64]{0:T(512)(128)(4,1)}, u32[]{:S(2)}) copy-start(pred[64]{0:T(512)(128)(4,1)} %copy-done.72) | copy-start | bytes 196
  186.0 5.5 %collective-permute-start.29 = (f32[16,128]{1,0:T(8,128)S(1)}, f32[16,128]{1,0:T(8,128)S(1)}, u32[]{:S(2)}, u32[]{:S(2)}) collective-permute-start(f32[16,128]{1,0:T(8,128)S(1)} %slice_bitcast_fusion.11), channel_id=1, source_target_pairs={{1,0},{2,1},{3,2},{5,4},{6,5},{7,6},{9,8},{10,9},{11,10},{13,12},{... | collective-permute-start | bytes 24584 | tf_op jit(solution)/shard_map/ppermute | solution.py:16
  196.9 1.2 copy-start.47
  199.3 6.1 %copy-start.71 = (f32[1,16,128]{2,1,0:T(8,128)S(1)}, f32[1,16,128]{2,1,0:T(8,128)}, u32[]{:S(2)}) copy-start(f32[1,16,128]{2,1,0:T(8,128)} %get-tuple-element.34) | copy-start | bytes 24580
  199.3 6.8 %copy-start.69 = (f32[1,16,128]{2,1,0:T(8,128)S(1)}, f32[1,16,128]{2,1,0:T(8,128)}, u32[]{:S(2)}) copy-start(f32[1,16,128]{2,1,0:T(8,128)} %copy-done.67) | copy-start | bytes 24580
  199.3 20.3 %copy-start.32 = (f32[64,16,128]{2,1,0:T(8,128)S(1)}, f32[64,16,128]{2,1,0:T(8,128)}, u32[]{:S(2)}) copy-start(f32[64,16,128]{2,1,0:T(8,128)} %copy-done.30) | copy-start | bytes 1572868
  199.3 20.3 %copy-start.35 = (f32[64,16,128]{2,1,0:T(8,128)S(1)}, f32[64,16,128]{2,1,0:T(8,128)}, u32[]{:S(2)}) copy-start(f32[64,16,128]{2,1,0:T(8,128)} %copy-done.33) | copy-start | bytes 1572868
  199.6 5.7 %collective-permute-start.30 = (f32[3,16,128]{2,1,0:T(8,128)S(1)}, f32[3,16,128]{2,1,0:T(8,128)S(1)}, u32[]{:S(2)}, u32[]{:S(2)}) collective-permute-start(f32[3,16,128]{2,1,0:T(8,128)S(1)} %pad_maximum_fusion.76), channel_id=1, source_target_pairs={{1,0},{2,1},{3,2},{5,4},{6,5},{7,6},{9,8},{10,9},{11,10},{13,12},{... | collective-permute-start | bytes 73736 | tf_op jit(solution)/shard_map/ppermute | solution.py:16
  (42 other events, 41.4 us)
where the time goes:
time: 222 us; the launch traced here: 221 us
  local copies, waits for them, and re-layouts  74.2 us (33%)
  waiting for transfers between devices  42.1 us (19%)
  blocking collectives  40.8 us (18%)
  other arithmetic  34.6 us (16%)
  starting transfers between devices  27 us (12%)
    all_gather x3, blocking collectives, shards(): lax.all_gather(jnp.stack([alpha_row, beta_row, gamma_row, rho_row])[None]...  40.8 us
    ppermute x7, waiting for transfers between devices, shifted(): return lax.ppermute(block, axis, route)  25.6 us
    slice x14, local copies, waits for them, and re-layouts, with_halo(): initial = lax.slice_in_dim(x, 0, width, axis=dim)  20.2 us
    unnamed x156, local copies, waits for them, and re-layouts  18.7 us
    ppermute x12, waiting for transfers between devices, with_halo(): before = lax.ppermute(last, axis, up)  10.2 us
    ppermute x6, local copies, waits for them, and re-layouts, with_halo(): before = lax.ppermute(last, axis, up)  10 us
    ppermute x6, local copies, waits for them, and re-layouts, with_halo(): after = lax.ppermute(initial, axis, down)  10 us
    slice x7, local copies, waits for them, and re-layouts, with_halo(): last = lax.slice_in_dim(x, length - width, length, axis=dim)  10 us
  transfers between devices with their start and end apart: 31, of which 24 were waited for; matrix products, arithmetic and copies ran while one was open for 15% of the time, Pallas kernels for 0%

commit v1 on v0

v1 whole, which is shorter than its diff:
```python
import functools

import jax
import jax.numpy as jnp
from jax import lax
from jax.experimental import pallas as pl
from jax.experimental.pallas import tpu as pltpu
from jax.sharding import PartitionSpec as P

SUBSTEPS = 3
CH = 0.3
GAIN = 4096.0
MESH = pl.DeviceIdType.MESH
GROUP = 16
F32 = jnp.float32


def kernel(
    K, nx, ny, nz,
    u_in, v_in, w_in, p_in, b_in, s_in,
    u_out, v_out, w_out, p_out,
    p, us, vs, w, s, bi, bj, E, D, H, X, Y, ps, h, uo, vo,
    i_low, i_high, i_from_up, i_from_down,
    j_own, j_from_left, j_from_right,
    hu, hbi, hv, hbj, C,
    cmine, cgath, fmine, fgath, red,
    in_sem, out_sem, hs_sem, hr_sem, cs_sem, cr_sem, ls_sem, lr_sem,
):
    gx, gy, me = lax.axis_index("gx"), lax.axis_index("gy"), lax.axis_index("lev")
    up, down = lax.rem(gx + 1, nx), lax.rem(gx + nx - 1, nx)
    right, left = lax.rem(gy + 1, ny), lax.rem(gy + ny - 1, ny)
    groups = K // GROUP
    K2, KJ = 2 * K, 8 * (K // GROUP)

    loads = []
    for n, (src, dst) in enumerate(
        ((p_in, p), (b_in, bi), (u_in, us), (v_in, vs), (s_in, s), (w_in, w))
    ):
        c = pltpu.make_async_copy(src, dst, in_sem.at[n])
        c.start()
        loads.append(c)

    barrier = pltpu.get_barrier_semaphore()
    for dev in (up, down):
        pl.semaphore_signal(barrier, inc=1, device_id={"gx": dev}, device_id_type=MESH)
    for dev in (left, right):
        pl.semaphore_signal(barrier, inc=1, device_id={"gy": dev}, device_id_type=MESH)
    for o in range(1, nz):
        pl.semaphore_signal(
            barrier, inc=1, device_id={"lev": lax.rem(me + o, nz)}, device_id_type=MESH
        )

    lane = lax.broadcasted_iota(jnp.int32, (8, 128), 1)
    sub = lax.broadcasted_iota(jnp.int32, (8, 128), 0)
    quad = lane % 4

    def roll(x, shift, axis):
        shift = shift % x.shape[axis]
        return x if shift == 0 else pltpu.roll(x, shift, axis)

    def at(ref, row, aligned=True):
        return ref[pl.ds(pl.multiple_of(row, 8) if aligned else row, 8), :]

    def put(ref, row, value):
        ref[pl.ds(pl.multiple_of(row, 8), 8), :] = value

    def each(body, carry=None, downward=False):
        def step(n, c):
            g = groups - 1 - n if downward else n
            return body(g, c)
        return lax.fori_loop(0, groups, step, carry)

    def pair(ref, g, j):
        return at(ref, g * 256 + 16 * j), at(ref, g * 256 + 16 * j + 8)

    def put_pair(ref, g, j, value):
        put(ref, g * 256 + 16 * j, value[0])
        put(ref, g * 256 + 16 * j + 8, value[1])

    def pack_edges(g, j, x, acc, ilo, ihi, f):
        row = 8 + f * K2 + g * 32 + 2 * j
        ilo[pl.ds(row, 2), :] = x[0][0:2]
        ihi[pl.ds(row, 2), :] = x[1][6:8]
        return pack_columns(j, x, acc)

    def pack_columns(j, x, acc):
        for half in range(2):
            q = 2 * j + half
            acc = jnp.where(lane // 4 == q, roll(x[half], 4 * q + 2, 1), acc)
        return acc

    zero = jnp.zeros((8, 128), F32)

    for c in loads[:4]:
        c.wait()

    def first_pack(g, carry):
        accp = accb = accv = zero
        for j in range(GROUP):
            accp = pack_edges(g, j, pair(p, g, j), accp, i_low.at[0], i_high.at[0], 0)
            xb = pair(bi, g, j)
            accb = pack_edges(g, j, xb, accb, i_low.at[0], i_high.at[0], 1)
            xu = pair(us, g, j)
            row = 8 + 2 * K2 + g * 32 + 2 * j
            i_low[0, pl.ds(row, 2), :] = xu[0][0:2]
            i_high[0, pl.ds(row, 2), :] = xu[1][6:8]
            accv = pack_columns(j, pair(vs, g, j), accv)
        j_own[0, pl.ds(pl.multiple_of(g * 8, 8), 8), :] = accp
        j_own[0, pl.ds(pl.multiple_of(KJ + g * 8, 8), 8), :] = accb
        j_own[0, pl.ds(pl.multiple_of(2 * KJ + g * 8, 8), 8), :] = accv
        return carry

    each(first_pack, 0)
    pl.semaphore_wait(barrier, 4 + nz - 1)

    def halo_copies(t):
        fields = 3 if t == 0 else 1
        ri, rj = pl.ds(8, fields * K2), pl.ds(0, fields * KJ)
        return [
            pltpu.make_async_remote_copy(
                src_ref=src.at[t, rows], dst_ref=dst.at[t, rows],
                send_sem=hs_sem.at[t, n], recv_sem=hr_sem.at[t, n],
                device_id={axis: dev}, device_id_type=MESH,
            )
            for n, (src, dst, rows, axis, dev) in enumerate((
                (j_own, j_from_left, rj, "gy", right),
                (j_own, j_from_right, rj, "gy", left),
                (i_low, i_from_up, ri, "gx", down),
                (i_high, i_from_down, ri, "gx", up),
            ))
        ]

    halos = halo_copies(0)
    for c in halos:
        c.start()

    def lev_copies(mine, gath, send, recv):
        return [
            pltpu.make_async_remote_copy(
                src_ref=mine, dst_ref=gath.at[me],
                send_sem=send.at[o - 1], recv_sem=recv.at[o - 1],
                device_id={"lev": lax.rem(me + o, nz)}, device_id_type=MESH,
            )
            for o in range(1, nz)
        ]

    loads[4].wait()

    def factor(g, carry):
        B, Z = carry
        for j in reversed(range(GROUP)):
            bb, ss = pair(bi, g, j), pair(s, g, j)
            newB, newZ = [], []
            for m in range(2):
                row = g * 256 + 16 * j + 8 * m
                gb = GAIN * bb[m]
                one = 1.0 + gb * B[m]
                d = 1.0 / (one + gb * ss[m])
                hh = gb * d
                e = hh * ss[m]
                put(D, row, d)
                put(H, row, hh)
                put(E, row, e)
                put(Y, row, hh * Z[m])
                newB.append(ss[m] * (one * d))
                newZ.append(e * Z[m])
            B, Z = tuple(newB), tuple(newZ)
        return B, Z

    one = jnp.ones((8, 128), F32)
    B, Z = each(factor, ((zero, zero), (one, one)), downward=True)

    def responses(g, carry):
        x, y = carry
        for j in range(GROUP):
            ee, hz = pair(E, g, j), pair(Y, g, j)
            x = tuple(ee[m] * x[m] for m in range(2))
            y = tuple(ee[m] * y[m] - hz[m] for m in range(2))
            put_pair(X, g, j, x)
            put_pair(Y, g, j, y)
        return x, y

    x, y = each(responses, ((one, one), (zero, zero)))
    for n, val in enumerate((x, y, Z, B)):
        for m in range(2):
            cmine[16 * n + 8 * m:16 * n + 8 * m + 8, :] = val[m]
            cgath[me, 16 * n + 8 * m:16 * n + 8 * m + 8, :] = val[m]
    consts = lev_copies(cmine, cgath, cs_sem, cr_sem)
    for c in consts:
        c.start()

    for c in halos:
        c.wait()

    def halo_rows(ref, t, f, g, j, sublane):
        return ref[t, pl.ds(8 + f * K2 + g * 32 + 2 * j - sublane, 8), :]

    def stagger(g, carry):
        rows = pl.multiple_of(g * 8, 8)
        vr = j_from_right[0, pl.ds(2 * KJ + rows, 8), :]
        br = j_from_right[0, pl.ds(KJ + rows, 8), :]
        for j in range(GROUP):
            xb, xu, xv = pair(bi, g, j), pair(us, g, j), pair(vs, g, j)
            for (val, dst, scale, f) in ((xu, us, 1.0, 2), (xb, bi, CH, 1)):
                r0, r1 = roll(val[0], 7, 0), roll(val[1], 7, 0)
                edge = halo_rows(i_from_up, 0, f, g, j, 7)
                put_pair(dst, g, j, (
                    scale * jnp.where(sub < 7, r0, r1), scale * jnp.where(sub < 7, r1, edge)
                ))
            for (val, dst, scale, packed) in ((xv, vs, 1.0, vr), (xb, bj, CH, br)):
                out = []
                for m in range(2):
                    q = 2 * j + m
                    out.append(scale * jnp.where(
                        lane == 127, roll(packed, 125 - 4 * q, 1), roll(val[m], 127, 1)
                    ))
                put_pair(dst, g, j, out)
        for r in range(4):
            row = g * 32 + 8 * r
            for (dst, f, scale) in ((hu, 2, 1.0), (hbi, 1, CH)):
                base = 8 + f * K2 + row
                below = i_from_down[0, pl.ds(base + 1, 8), :]
                own = i_low[0, pl.ds(base - 1, 8), :]
                put(dst, 8 + row, scale * jnp.where(sub % 2 == 0, below, own))
        for (dst, f, scale) in ((hv, 2, 1.0), (hbj, 1, CH)):
            fl = j_from_left[0, pl.ds(f * KJ + rows, 8), :]
            own = j_own[0, pl.ds(f * KJ + rows, 8), :]
            put(dst, rows, scale * roll(jnp.where(quad == 1, fl, own), 1, 1))
        return carry

    each(stagger, 0)

    for c in consts:
        c.wait()

    def crow(d, n):
        return cgath[d, 16 * n:16 * n + 16, :]

    beta = crow(nz - 1, 3)
    red[nz - 1, 0:16, :] = beta
    for d in range(nz - 2, -1, -1):
        R = 1.0 / (1.0 - crow(d, 1) * beta)
        zbr = crow(d, 2) * beta * R
        red[d, 16:32, :] = R
        red[d, 32:48, :] = zbr
        beta = crow(d, 3) + zbr * crow(d, 0)
        red[d, 0:16, :] = beta

    loads[5].wait()

    outs = []
    for t in range(SUBSTEPS):
        final = t == SUBSTEPS - 1
        if t > 0:
            for c in halos:
                c.wait()

        def explicit(g, A):
            rows = pl.multiple_of(g * 8, 8)
            for r in range(4):
                row = g * 32 + 8 * r
                low = i_low[t, pl.ds(pl.multiple_of(8 + row, 8), 8), :]
                below = i_from_down[t, pl.ds(pl.multiple_of(8 + row, 8), 8), :]
                put(hu, 8 + row, at(hu, 8 + row) - at(hbi, 8 + row) * (low - below))
            own = j_own[t, pl.ds(rows, 8), :]
            fl = j_from_left[t, pl.ds(rows, 8), :]
            fr = j_from_right[t, pl.ds(rows, 8), :]
            hv_new = at(hv, rows) - at(hbj, rows) * (own - roll(fl, 2, 1))
            put(hv, rows, hv_new)
            c = jnp.where(quad < 2, roll(fr, 126, 1), hv_new)
            for j in reversed(range(GROUP)):
                pp, uu, vv, ww = pair(p, g, j), pair(us, g, j), pair(vs, g, j), pair(w, g, j)
                bbi, bbj, ss = pair(bi, g, j), pair(bj, g, j), pair(s, g, j)
                ee, dd, hh = pair(E, g, j), pair(D, g, j), pair(H, g, j)
                r0, r1 = roll(pp[0], 6, 0), roll(pp[1], 6, 0)
                edge = halo_rows(i_from_up, t, 0, g, j, 6)
                pi = (jnp.where(sub < 6, r0, r1), jnp.where(sub < 6, r1, edge))
                un = tuple(uu[m] - bbi[m] * (pi[m] - pp[m]) for m in range(2))
                put_pair(us, g, j, un)
                r0, r1 = roll(un[0], 2, 0), roll(un[1], 2, 0)
                edge = at(hu, 8 + g * 32 + 2 * j, False)
                um = (jnp.where(sub < 2, edge, r0), jnp.where(sub < 2, r0, r1))
                newA, hs, pss, vn = [], [], [], []
                for m in range(2):
                    edge = roll(c, 126 - 4 * (2 * j + m), 1)
                    pj = jnp.where(lane >= 126, edge, roll(pp[m], 126, 1))
                    v_new = vv[m] - bbj[m] * (pj - pp[m])
                    vm = jnp.where(lane < 2, edge, roll(v_new, 2, 1))
                    star = pp[m] - (CH * ss[m]) * ((un[m] - um[m]) + (v_new - vm))
                    dw = dd[m] * ww[m]
                    hs.append(dw + hh[m] * (star - A[m]))
                    newA.append(ee[m] * A[m] + ((star - ee[m] * star) - ss[m] * dw))
                    pss.append(star)
                    vn.append(v_new)
                put_pair(vs, g, j, vn)
                put_pair(ps, g, j, pss)
                put_pair(h, g, j, hs)
                A = tuple(newA)
            return A

        A = each(explicit, (zero, zero), downward=True)

        def forward(g, x):
            for j in range(GROUP):
                ee, hh = pair(E, g, j), pair(h, g, j)
                x = tuple(ee[m] * x[m] + hh[m] for m in range(2))
                put_pair(w, g, j, x)
            return x

        x = each(forward, (zero, zero))
        for n, val in enumerate((A, x)):
            for m in range(2):
                fmine[t, 16 * n + 8 * m:16 * n + 8 * m + 8, :] = val[m]
                fgath[t, me, 16 * n + 8 * m:16 * n + 8 * m + 8, :] = val[m]
        sends = lev_copies(fmine.at[t], fgath.at[t], ls_sem.at[t], lr_sem.at[t])
        for c in sends:
            c.start()

        if final:
            def emit(g, carry):
                hvg = at(hv, pl.multiple_of(g * 8, 8))
                for j in range(GROUP):
                    uu, vv = pair(us, g, j), pair(vs, g, j)
                    r0, r1 = roll(uu[0], 1, 0), roll(uu[1], 1, 0)
                    edge = at(hu, 8 + g * 32 + 2 * j + 1, False)
                    put_pair(uo, g, j, (jnp.where(sub < 1, edge, r0), jnp.where(sub < 1, r0, r1)))
                    put_pair(vo, g, j, [
                        jnp.where(
                            lane == 0, roll(hvg, 125 - 4 * (2 * j + m), 1), roll(vv[m], 1, 1)
                        )
                        for m in range(2)
                    ])
                return carry

            each(emit, 0)
            for n, (src, dst) in enumerate(((uo, u_out), (vo, v_out))):
                c = pltpu.make_async_copy(src, dst, out_sem.at[n])
                c.start()
                outs.append(c)

        for c in sends:
            c.wait()

        alphas = [None] * nz
        alpha = fgath[t, nz - 1, 0:16, :]
        alphas[nz - 1] = alpha
        sums = [None] * nz
        for d in range(nz - 2, -1, -1):
            sums[d] = fgath[t, d, 16:32, :] + crow(d, 1) * alpha
            alpha = fgath[t, d, 0:16, :] + crow(d, 2) * alpha + red[d, 32:48, :] * sums[d]
            alphas[d] = alpha
        nothing = jnp.zeros((16, 128), F32)
        wb = pa = nothing
        below = nothing
        for d in range(nz):
            wb = jnp.where(me == d, below, wb)
            if d < nz - 1:
                below = red[d, 16:32, :] * (sums[d] + crow(d, 0) * below)
                above = alphas[d + 1] + red[d + 1, 0:16, :] * below
                pa = jnp.where(me == d, above, pa)
        wb2, pa2 = (wb[0:8], wb[8:16]), (pa[0:8], pa[8:16])

        def implicit(g, wprev):
            acc = zero
            for j in range(GROUP):
                w0, xx, yy = pair(w, g, j), pair(X, g, j), pair(Y, g, j)
                ss, star = pair(s, g, j), pair(ps, g, j)
                wn = tuple(w0[m] + xx[m] * wb2[m] + yy[m] * pa2[m] for m in range(2))
                pn = tuple(star[m] - ss[m] * (wn[m] - wprev[m]) for m in range(2))
                put_pair(w, g, j, wn)
                put_pair(p, g, j, pn)
                if not final:
                    acc = pack_edges(g, j, pn, acc, i_low.at[t + 1], i_high.at[t + 1], 0)
                wprev = wn
            if not final:
                j_own[t + 1, pl.ds(pl.multiple_of(g * 8, 8), 8), :] = acc
            return wprev

        each(implicit, wb2)
        if not final:
            halos = halo_copies(t + 1)
            for c in halos:
                c.start()

    for n, (src, dst) in enumerate(((w, w_out), (p, p_out))):
        c = pltpu.make_async_copy(src, dst, out_sem.at[2 + n])
        c.start()
        outs.append(c)
    for c in outs:
        c.wait()


def solution(mesh):
    nx, ny, nz = (mesh.shape[a] for a in ("gx", "gy", "lev"))

    def shards(*fields):
        K, I, J = fields[0].shape
        assert I == 16 and J == 128 and K % GROUP == 0
        R, KJ, T = K * I, 8 * (K // GROUP), SUBSTEPS
        full = pltpu.VMEM((R, J), F32)
        ihalo = pltpu.VMEM((T, 6 * K + 16, J), F32)
        jhalo = pltpu.VMEM((T, 3 * KJ, J), F32)
        outs = pl.pallas_call(
            functools.partial(kernel, K, nx, ny, nz),
            out_shape=[jax.ShapeDtypeStruct((R, J), F32)] * 4,
            in_specs=[pl.BlockSpec(memory_space=pl.ANY)] * 6,
            out_specs=[pl.BlockSpec(memory_space=pl.ANY)] * 4,
            scratch_shapes=[full] * 16 + [ihalo] * 4 + [jhalo] * 3 + [
                pltpu.VMEM((2 * K + 16, J), F32),
                pltpu.VMEM((2 * K + 16, J), F32),
                pltpu.VMEM((KJ, J), F32),
                pltpu.VMEM((KJ, J), F32),
                pltpu.VMEM((KJ, J), F32),
                pltpu.VMEM((64, J), F32),
                pltpu.VMEM((nz, 64, J), F32),
                pltpu.VMEM((T, 32, J), F32),
                pltpu.VMEM((T, nz, 32, J), F32),
                pltpu.VMEM((nz, 48, J), F32),
                pltpu.SemaphoreType.DMA((6,)),
                pltpu.SemaphoreType.DMA((4,)),
                pltpu.SemaphoreType.DMA((T, 4)),
                pltpu.SemaphoreType.DMA((T, 4)),
                pltpu.SemaphoreType.DMA((max(nz - 1, 1),)),
                pltpu.SemaphoreType.DMA((max(nz - 1, 1),)),
                pltpu.SemaphoreType.DMA((T, max(nz - 1, 1))),
                pltpu.SemaphoreType.DMA((T, max(nz - 1, 1))),
            ],
            compiler_params=pltpu.CompilerParams(collective_id=0, has_side_effects=True),
        )(*(f.reshape(R, J) for f in fields))
        return tuple(o.reshape(K, I, J) for o in outs)

    spec = P("lev", "gx", "gy")
    return jax.shard_map(
        shards, mesh=mesh, in_specs=(spec,) * 6, out_specs=(spec,) * 4, check_vma=False
    )
```

time: 222 us -> 41.4 us (0.19)
  local copies, waits for them, and re-layouts: 74.2 us -> 5.18 us
  waiting for transfers between devices: 42.1 us -> 0 us
  blocking collectives: 40.8 us -> 0 us
  Pallas kernels: 0 us -> 35.3 us
  other arithmetic: 34.6 us -> 0 us
  starting transfers between devices: 27 us -> 0 us
    ppermute x31 -> x0, waiting for transfers between devices: 42.1 us -> none  [the longest x7 25.6 us: shifted(): return lax.ppermute(block, axis, route)]
    all_gather x3 -> x0, blocking collectives: 40.8 us -> none  [shards(): lax.all_gather(jnp.stack([alpha_row, beta_row, gamma_row, rho_row])[None]...]
    pallas_call x0 -> x1, Pallas kernels: none -> 35.3 us  [shards(): pl.pallas_call(functools.partial(kernel, K, nx, ny, nz), out_shape=[jax.S...]
    slice x80 -> x0, local copies, waits for them, and re-layouts: 33.5 us -> none  [the longest x14 20.2 us: with_halo(): initial = lax.slice_in_dim(x, 0, width, axis=dim)]
    ppermute x31 -> x0, starting transfers between devices: 27 us -> none  [the longest x12 9.51 us: with_halo(): before = lax.ppermute(last, axis, up)]
    sub x31 -> x0, other arithmetic: 23.9 us -> none  [the longest x3 7.65 us: shards(): p_star = pressure - courant_h * stiffness * divergence]
    ppermute x12 -> x0, local copies, waits for them, and re-layouts: 20.1 us -> none  [the longest x6 10 us: with_halo(): before = lax.ppermute(last, axis, up)]
    unnamed x156 -> x10, local copies, waits for them, and re-layouts: 18.7 us -> 5.18 us
  transfers between devices with their start and end apart: 31 -> 0, of which waited for: 24 -> 0; matrix products, arithmetic and copies ran while one was open for 15% -> 0% of each run, Pallas kernels for 0% -> 0%
where the time goes in v1:
time: 41.4 us; the launch traced here: 41.2 us
  Pallas kernels  35.3 us (85%)
  local copies, waits for them, and re-layouts  5.18 us (13%)
  between operations  0.65 us (2%)
    pallas_call x1, Pallas kernels, shards(): pl.pallas_call(functools.partial(kernel, K, nx, ny, nz), out_shape=[jax.S...  35.3 us
    unnamed x10, local copies, waits for them, and re-layouts  5.18 us

profile of v1, /device:TPU:0, one launch (start us, length us, event | category | flops | bytes accessed | tf_op | source)
XLA Modules:
  0.0 41.2 jit_solution(10667137848075514574)
XLA Ops:
  0.6 35.3 %shard_map.93 = (f32[1024,128]{1,0:T(8,128)}, f32[1024,128]{1,0:T(8,128)}, f32[1024,128]{1,0:T(8,128)}, f32[1024,128]{1,0:T(8,128)}) custom-call(f32[1024,128]{1,0:T(8,128)} %bitcast.14, f32[1024,128]{1,0:T(8,128)} %bitcast.15, f32[1024,128]{1,0:T(8,128)} %bitcast.16, f32[1024,128]{1,0:T(8,128)} %bitcast.17, f32[1024,128]{1,0:T(8,128)} %bitcast.18, ...), custom_call_target="tpu_custom_call" | custom-call | tf_op jit(solution)/shard_map/pallas_call | solution.py:403
  36.0 0.0 copy-start.2
  36.0 1.9 %copy.14 = f32[64,16,128]{2,1,0:T(8,128)} copy(f32[64,16,128]{2,1,0:T(8,128)} %bitcast.13) | data formatting | bytes 1048576
  37.9 0.0 copy-done.2
  37.9 0.0 copy-start.1
  37.9 0.8 %copy.15 = f32[64,16,128]{2,1,0:T(8,128)} copy(f32[64,16,128]{2,1,0:T(8,128)S(1)} %bitcast.12) | data formatting | bytes 1048576
  38.7 0.4 %copy-done.1 = f32[1024,128]{1,0:T(8,128)S(1)} copy-done((f32[1024,128]{1,0:T(8,128)S(1)}, f32[1024,128]{1,0:T(8,128)}, u32[]{:S(2)}) %copy-start.1) | copy-done | bytes 524312
  39.2 0.0 copy-start
  39.2 0.8 %copy.16 = f32[64,16,128]{2,1,0:T(8,128)} copy(f32[64,16,128]{2,1,0:T(8,128)S(1)} %bitcast.11) | data formatting | bytes 1048576
  40.0 0.4 %copy-done = f32[1024,128]{1,0:T(8,128)S(1)} copy-done((f32[1024,128]{1,0:T(8,128)S(1)}, f32[1024,128]{1,0:T(8,128)}, u32[]{:S(2)}) %copy-start) | copy-done | bytes 524312
  40.4 0.8 %copy.17 = f32[64,16,128]{2,1,0:T(8,128)} copy(f32[64,16,128]{2,1,0:T(8,128)S(1)} %bitcast.10) | data formatting | bytes 1048576
Async XLA Ops:
  36.0 1.9 %copy-start.2 = (f32[1024,128]{1,0:T(8,128)S(1)}, f32[1024,128]{1,0:T(8,128)}, u32[]{:S(2)}) copy-start(f32[1024,128]{1,0:T(8,128)} %get-tuple-element.9) | copy-start | bytes 1572868
  37.9 1.2 %copy-start.1 = (f32[1024,128]{1,0:T(8,128)S(1)}, f32[1024,128]{1,0:T(8,128)}, u32[]{:S(2)}) copy-start(f32[1024,128]{1,0:T(8,128)} %get-tuple-element.10) | copy-start | bytes 1572868
  39.2 1.2 %copy-start = (f32[1024,128]{1,0:T(8,128)S(1)}, f32[1024,128]{1,0:T(8,128)}, u32[]{:S(2)}) copy-start(f32[1024,128]{1,0:T(8,128)} %get-tuple-element.11) | copy-start | bytes 1572868

commit v2 on v1

--- a/solution.py
+++ b/solution.py
@@ -18,19 +18,19 @@
 def kernel(
     K, nx, ny, nz,
     u_in, v_in, w_in, p_in, b_in, s_in,
-    u_out, v_out, w_out, p_out,
-    p, us, vs, w, s, bi, bj, E, D, H, X, Y, ps, h, uo, vo,
+    uo, vo, w, p,
+    us, vs, s, bi, bj, E, D, H, X, Y, ps, h,
     i_low, i_high, i_from_up, i_from_down,
-    j_own, j_from_left, j_from_right,
-    hu, hbi, hv, hbj, C,
-    cmine, cgath, fmine, fgath, red,
-    in_sem, out_sem, hs_sem, hr_sem, cs_sem, cr_sem, ls_sem, lr_sem,
+    j_own, j_to_right, j_to_left, j_from_left, j_from_right,
+    hu, hbi, hv, hbj, C, vbr,
+    cmine, cgath, fmine, fgath, red, mine,
+    in_sem, hs_sem, hr_sem, cs_sem, cr_sem, ls_sem, lr_sem,
 ):
     gx, gy, me = lax.axis_index("gx"), lax.axis_index("gy"), lax.axis_index("lev")
     up, down = lax.rem(gx + 1, nx), lax.rem(gx + nx - 1, nx)
     right, left = lax.rem(gy + 1, ny), lax.rem(gy + ny - 1, ny)
     groups = K // GROUP
-    K2, KJ = 2 * K, 8 * (K // GROUP)
+    K2, KJ, KH = 2 * K, 8 * (K // GROUP), 4 * (K // GROUP)
 
     loads = []
     for n, (src, dst) in enumerate(
@@ -111,11 +111,30 @@
         return carry
 
     each(first_pack, 0)
+
+    def dense(t, f):
+        for n in range(groups // 2):
+            a, b = (j_own[t, 16 * n + 8 * m:16 * n + 8 * m + 8, :] for m in range(2))
+            j_to_right[t, 8 * n:8 * n + 8, :] = jnp.where(quad < 2, a, roll(b, 2, 1))
+            j_to_left[t, 8 * n:8 * n + 8, :] = jnp.where(quad < 2, roll(a, -2, 1), b)
+            if f:
+                rights, lefts = [], []
+                for m in range(2):
+                    k = 16 * n + 8 * m
+                    ab = j_own[t, KJ + k:KJ + k + 8, :]
+                    av = j_own[t, 2 * KJ + k:2 * KJ + k + 8, :]
+                    rights.append(jnp.where(quad == 0, roll(av, -1, 1), ab))
+                    lefts.append(jnp.where(quad == 0, roll(av, -2, 1), roll(ab, -1, 1)))
+                k = KH + 8 * n
+                for ref, (a, b) in ((j_to_right, rights), (j_to_left, lefts)):
+                    ref[t, k:k + 8, :] = jnp.where(quad < 2, a, roll(b, 2, 1))
+
+    dense(0, True)
     pl.semaphore_wait(barrier, 4 + nz - 1)
 
     def halo_copies(t):
-        fields = 3 if t == 0 else 1
-        ri, rj = pl.ds(8, fields * K2), pl.ds(0, fields * KJ)
+        ri = pl.ds(8, (3 if t == 0 else 1) * K2)
+        rj = pl.ds(0, (2 if t == 0 else 1) * KH)
         return [
             pltpu.make_async_remote_copy(
                 src_ref=src.at[t, rows], dst_ref=dst.at[t, rows],
@@ -123,8 +142,8 @@
                 device_id={axis: dev}, device_id_type=MESH,
             )
             for n, (src, dst, rows, axis, dev) in enumerate((
-                (j_own, j_from_left, rj, "gy", right),
-                (j_own, j_from_right, rj, "gy", left),
+                (j_to_right, j_from_left, rj, "gy", right),
+                (j_to_left, j_from_right, rj, "gy", left),
                 (i_low, i_from_up, ri, "gx", down),
                 (i_high, i_from_down, ri, "gx", up),
             ))
@@ -134,10 +153,10 @@
     for c in halos:
         c.start()
 
-    def lev_copies(mine, gath, send, recv):
+    def lev_copies(src, gath, send, recv):
         return [
             pltpu.make_async_remote_copy(
-                src_ref=mine, dst_ref=gath.at[me],
+                src_ref=src(lax.div(me + o, nz)), dst_ref=gath.at[me],
                 send_sem=send.at[o - 1], recv_sem=recv.at[o - 1],
                 device_id={"lev": lax.rem(me + o, nz)}, device_id_type=MESH,
             )
@@ -185,20 +204,33 @@
         for m in range(2):
             cmine[16 * n + 8 * m:16 * n + 8 * m + 8, :] = val[m]
             cgath[me, 16 * n + 8 * m:16 * n + 8 * m + 8, :] = val[m]
-    consts = lev_copies(cmine, cgath, cs_sem, cr_sem)
+    consts = lev_copies(lambda below: cmine, cgath, cs_sem, cr_sem)
     for c in consts:
         c.start()
 
+    def crow(d, n):
+        return cgath[d, 16 * n:16 * n + 16, :]
+
     for c in halos:
         c.wait()
 
     def halo_rows(ref, t, f, g, j, sublane):
         return ref[t, pl.ds(8 + f * K2 + g * 32 + 2 * j - sublane, 8), :]
 
+    for n in range(groups // 2):
+        fr = j_from_right[0, KH + 8 * n:KH + 8 * n + 8, :]
+        fl = j_from_left[0, KH + 8 * n:KH + 8 * n + 8, :]
+        for m in range(2):
+            k = 16 * n + 8 * m
+            vbr[k:k + 8, :] = roll(fr, -2 * m, 1)
+            flg = roll(fl, -2 * m, 1)
+            ab = j_own[0, KJ + k:KJ + k + 8, :]
+            av = j_own[0, 2 * KJ + k:2 * KJ + k + 8, :]
+            hv[k:k + 8, :] = jnp.where(quad == 2, roll(flg, 2, 1), roll(av, 1, 1))
+            hbj[k:k + 8, :] = CH * roll(jnp.where(quad == 1, flg, ab), 1, 1)
+
     def stagger(g, carry):
-        rows = pl.multiple_of(g * 8, 8)
-        vr = j_from_right[0, pl.ds(2 * KJ + rows, 8), :]
-        br = j_from_right[0, pl.ds(KJ + rows, 8), :]
+        packed = at(vbr, g * 8)
         for j in range(GROUP):
             xb, xu, xv = pair(bi, g, j), pair(us, g, j), pair(vs, g, j)
             for (val, dst, scale, f) in ((xu, us, 1.0, 2), (xb, bi, CH, 1)):
@@ -207,12 +239,12 @@
                 put_pair(dst, g, j, (
                     scale * jnp.where(sub < 7, r0, r1), scale * jnp.where(sub < 7, r1, edge)
                 ))
-            for (val, dst, scale, packed) in ((xv, vs, 1.0, vr), (xb, bj, CH, br)):
+            for (val, dst, scale, first) in ((xv, vs, 1.0, 127), (xb, bj, CH, 126)):
                 out = []
                 for m in range(2):
                     q = 2 * j + m
                     out.append(scale * jnp.where(
-                        lane == 127, roll(packed, 125 - 4 * q, 1), roll(val[m], 127, 1)
+                        lane == 127, roll(packed, first - 4 * q, 1), roll(val[m], 127, 1)
                     ))
                 put_pair(dst, g, j, out)
         for r in range(4):
@@ -222,52 +254,36 @@
                 below = i_from_down[0, pl.ds(base + 1, 8), :]
                 own = i_low[0, pl.ds(base - 1, 8), :]
                 put(dst, 8 + row, scale * jnp.where(sub % 2 == 0, below, own))
-        for (dst, f, scale) in ((hv, 2, 1.0), (hbj, 1, CH)):
-            fl = j_from_left[0, pl.ds(f * KJ + rows, 8), :]
-            own = j_own[0, pl.ds(f * KJ + rows, 8), :]
-            put(dst, rows, scale * roll(jnp.where(quad == 1, fl, own), 1, 1))
         return carry
 
     each(stagger, 0)
 
-    for c in consts:
-        c.wait()
-
-    def crow(d, n):
-        return cgath[d, 16 * n:16 * n + 16, :]
-
-    beta = crow(nz - 1, 3)
-    red[nz - 1, 0:16, :] = beta
-    for d in range(nz - 2, -1, -1):
-        R = 1.0 / (1.0 - crow(d, 1) * beta)
-        zbr = crow(d, 2) * beta * R
-        red[d, 16:32, :] = R
-        red[d, 32:48, :] = zbr
-        beta = crow(d, 3) + zbr * crow(d, 0)
-        red[d, 0:16, :] = beta
-
     loads[5].wait()
 
-    outs = []
     for t in range(SUBSTEPS):
         final = t == SUBSTEPS - 1
         if t > 0:
             for c in halos:
                 c.wait()
 
+        for n in range(groups // 2):
+            fr = j_from_right[t, 8 * n:8 * n + 8, :]
+            fl = j_from_left[t, 8 * n:8 * n + 8, :]
+            for m in range(2):
+                k = 16 * n + 8 * m
+                before = roll(fl, 2, 1) if m == 0 else fl
+                own = j_own[t, k:k + 8, :]
+                hv_new = hv[k:k + 8, :] - hbj[k:k + 8, :] * (own - before)
+                hv[k:k + 8, :] = hv_new
+                C[k:k + 8, :] = jnp.where(quad < 2, roll(fr, -2 * m, 1), hv_new)
+
         def explicit(g, A):
-            rows = pl.multiple_of(g * 8, 8)
             for r in range(4):
                 row = g * 32 + 8 * r
                 low = i_low[t, pl.ds(pl.multiple_of(8 + row, 8), 8), :]
                 below = i_from_down[t, pl.ds(pl.multiple_of(8 + row, 8), 8), :]
                 put(hu, 8 + row, at(hu, 8 + row) - at(hbi, 8 + row) * (low - below))
-            own = j_own[t, pl.ds(rows, 8), :]
-            fl = j_from_left[t, pl.ds(rows, 8), :]
-            fr = j_from_right[t, pl.ds(rows, 8), :]
-            hv_new = at(hv, rows) - at(hbj, rows) * (own - roll(fl, 2, 1))
-            put(hv, rows, hv_new)
-            c = jnp.where(quad < 2, roll(fr, 126, 1), hv_new)
+            c = at(C, g * 8)
             for j in reversed(range(GROUP)):
                 pp, uu, vv, ww = pair(p, g, j), pair(us, g, j), pair(vs, g, j), pair(w, g, j)
                 bbi, bbj, ss = pair(bi, g, j), pair(bj, g, j), pair(s, g, j)
@@ -308,11 +324,43 @@
             return x
 
         x = each(forward, (zero, zero))
-        for n, val in enumerate((A, x)):
-            for m in range(2):
-                fmine[t, 16 * n + 8 * m:16 * n + 8 * m + 8, :] = val[m]
-                fgath[t, me, 16 * n + 8 * m:16 * n + 8 * m + 8, :] = val[m]
-        sends = lev_copies(fmine.at[t], fgath.at[t], ls_sem.at[t], lr_sem.at[t])
+        if t == 0:
+            for c in consts:
+                c.wait()
+            nothing = jnp.zeros((16, 128), F32)
+            picks = {name: nothing for name in ("psi", "r2", "beta", "r", "wa", "aw", "lam")}
+
+            def pick(name, d, val):
+                picks[name] = jnp.where(me == d, val, picks[name])
+
+            beta = nothing
+            betas = [None] * nz
+            for d in range(nz - 1, -1, -1):
+                R = 1.0 / (1.0 - crow(d, 1) * beta)
+                zbr = crow(d, 2) * beta * R
+                lam = crow(d, 2) + zbr * crow(d, 1)
+                red[d, 0:16, :] = lam
+                for name, val in (("beta", beta), ("r", R), ("aw", zbr), ("lam", lam)):
+                    pick(name, d, val)
+                beta = crow(d, 3) + zbr * crow(d, 0)
+                betas[d] = beta
+            psi = nothing
+            for d in range(nz):
+                xr = crow(d, 0) / (1.0 - psi * crow(d, 3))
+                xrp = xr * psi
+                red[d, 16:32, :] = xr
+                pick("psi", d, psi)
+                pick("r2", d, 1.0 / (1.0 - psi * betas[d]))
+                pick("wa", d, xrp)
+                psi = crow(d, 1) + xrp * crow(d, 2)
+            for n, name in enumerate(picks):
+                mine[16 * n:16 * n + 16, :] = picks[name]
+
+        psi, r2, beta, r, wa, aw, lam = (mine[16 * n:16 * n + 16, :] for n in range(7))
+        A0, W0 = (jnp.concatenate(q, 0) for q in (A, x))
+        up_row, down_row = W0 + wa * A0, A0 + aw * W0
+        fmine[t, 0], fmine[t, 1] = up_row, down_row
+        sends = lev_copies(lambda below: fmine.at[t, below], fgath.at[t], ls_sem.at[t], lr_sem.at[t])
         for c in sends:
             c.start()
 
@@ -333,31 +381,16 @@
                 return carry
 
             each(emit, 0)
-            for n, (src, dst) in enumerate(((uo, u_out), (vo, v_out))):
-                c = pltpu.make_async_copy(src, dst, out_sem.at[n])
-                c.start()
-                outs.append(c)
-
         for c in sends:
             c.wait()
 
-        alphas = [None] * nz
-        alpha = fgath[t, nz - 1, 0:16, :]
-        alphas[nz - 1] = alpha
-        sums = [None] * nz
-        for d in range(nz - 2, -1, -1):
-            sums[d] = fgath[t, d, 16:32, :] + crow(d, 1) * alpha
-            alpha = fgath[t, d, 0:16, :] + crow(d, 2) * alpha + red[d, 32:48, :] * sums[d]
-            alphas[d] = alpha
-        nothing = jnp.zeros((16, 128), F32)
-        wb = pa = nothing
-        below = nothing
-        for d in range(nz):
-            wb = jnp.where(me == d, below, wb)
-            if d < nz - 1:
-                below = red[d, 16:32, :] * (sums[d] + crow(d, 0) * below)
-                above = alphas[d + 1] + red[d + 1, 0:16, :] * below
-                pa = jnp.where(me == d, above, pa)
+        omega = alpha = jnp.zeros((16, 128), F32)
+        for d in range(nz - 1):
+            omega = jnp.where(me > d, fgath[t, d] + red[d, 16:32, :] * omega, omega)
+        for d in range(nz - 1, 0, -1):
+            alpha = jnp.where(me < d, fgath[t, d] + red[d, 0:16, :] * alpha, alpha)
+        wb = r2 * (omega + psi * (down_row + lam * alpha))
+        pa = alpha + beta * (r * (W0 + crow(me, 1) * alpha + crow(me, 0) * wb))
         wb2, pa2 = (wb[0:8], wb[8:16]), (pa[0:8], pa[8:16])
 
         def implicit(g, wprev):
@@ -378,15 +411,20 @@
 
         each(implicit, wb2)
         if not final:
+            dense(t + 1, False)
             halos = halo_copies(t + 1)
             for c in halos:
                 c.start()
 
-    for n, (src, dst) in enumerate(((w, w_out), (p, p_out))):
-        c = pltpu.make_async_copy(src, dst, out_sem.at[2 + n])
+
+def store(u, v, w, p, u_out, v_out, w_out, p_out, sem):
+    copies = [
+        pltpu.make_async_copy(src, dst, sem.at[n])
+        for n, (src, dst) in enumerate(((u, u_out), (v, v_out), (w, w_out), (p, p_out)))
+    ]
+    for c in copies:
         c.start()
-        outs.append(c)
-    for c in outs:
+    for c in copies:
         c.wait()
 
 
@@ -395,29 +433,31 @@
 
     def shards(*fields):
         K, I, J = fields[0].shape
-        assert I == 16 and J == 128 and K % GROUP == 0
+        assert I == 16 and J == 128 and K % (2 * GROUP) == 0
         R, KJ, T = K * I, 8 * (K // GROUP), SUBSTEPS
         full = pltpu.VMEM((R, J), F32)
         ihalo = pltpu.VMEM((T, 6 * K + 16, J), F32)
         jhalo = pltpu.VMEM((T, 3 * KJ, J), F32)
+        jdense = pltpu.VMEM((T, KJ, J), F32)
         outs = pl.pallas_call(
             functools.partial(kernel, K, nx, ny, nz),
-            out_shape=[jax.ShapeDtypeStruct((R, J), F32)] * 4,
+            out_shape=[full] * 4,
             in_specs=[pl.BlockSpec(memory_space=pl.ANY)] * 6,
-            out_specs=[pl.BlockSpec(memory_space=pl.ANY)] * 4,
-            scratch_shapes=[full] * 16 + [ihalo] * 4 + [jhalo] * 3 + [
+            out_specs=[pl.BlockSpec(memory_space=pltpu.VMEM)] * 4,
+            scratch_shapes=[full] * 12 + [ihalo] * 4 + [jhalo] + [jdense] * 4 + [
                 pltpu.VMEM((2 * K + 16, J), F32),
                 pltpu.VMEM((2 * K + 16, J), F32),
                 pltpu.VMEM((KJ, J), F32),
                 pltpu.VMEM((KJ, J), F32),
                 pltpu.VMEM((KJ, J), F32),
+                pltpu.VMEM((KJ, J), F32),
                 pltpu.VMEM((64, J), F32),
                 pltpu.VMEM((nz, 64, J), F32),
-                pltpu.VMEM((T, 32, J), F32),
-                pltpu.VMEM((T, nz, 32, J), F32),
-                pltpu.VMEM((nz, 48, J), F32),
+                pltpu.VMEM((T, 2, 16, J), F32),
+                pltpu.VMEM((T, nz, 16, J), F32),
+                pltpu.VMEM((nz, 32, J), F32),
+                pltpu.VMEM((112, J), F32),
                 pltpu.SemaphoreType.DMA((6,)),
-                pltpu.SemaphoreType.DMA((4,)),
                 pltpu.SemaphoreType.DMA((T, 4)),
                 pltpu.SemaphoreType.DMA((T, 4)),
                 pltpu.SemaphoreType.DMA((max(nz - 1, 1),)),
@@ -427,6 +467,13 @@
             ],
             compiler_params=pltpu.CompilerParams(collective_id=0, has_side_effects=True),
         )(*(f.reshape(R, J) for f in fields))
+        outs = pl.pallas_call(
+            store,
+            out_shape=[jax.ShapeDtypeStruct((R, J), F32)] * 4,
+            in_specs=[pl.BlockSpec(memory_space=pltpu.VMEM)] * 4,
+            out_specs=[pl.BlockSpec(memory_space=pl.ANY)] * 4,
+            scratch_shapes=[pltpu.SemaphoreType.DMA((4,))],
+        )(*(pltpu.with_memory_space_constraint(o, pltpu.VMEM) for o in outs))
         return tuple(o.reshape(K, I, J) for o in outs)
 
     spec = P("lev", "gx", "gy")

time: 41.4 us -> 35 us (0.85)
  local copies, waits for them, and re-layouts: 5.18 us -> 0 us
  Pallas kernels: 35.3 us -> 34.2 us
    unnamed x10 -> x0, local copies, waits for them, and re-layouts: 5.18 us -> none
    pallas_call x1 -> x2, Pallas kernels: 35.3 us -> 34.2 us  [the longest x1 32.9 us: shards(): pl.pallas_call(functools.partial(kernel, K, nx, ny, nz), out_shape=[full]...]
where the time goes in v2:
time: 35 us; the launch traced here: 34.9 us
  Pallas kernels  34.2 us (98%)
  between operations  0.64 us (2%)
    pallas_call x1, Pallas kernels, shards(): pl.pallas_call(functools.partial(kernel, K, nx, ny, nz), out_shape=[full]...  32.9 us
    pallas_call x1, Pallas kernels, shards(): pl.pallas_call(store, out_shape=[jax.ShapeDtypeStruct((R, J), F32)] * 4,...  1.35 us

profile of v2, /device:TPU:0, one launch (start us, length us, event | category | flops | bytes accessed | tf_op | source)
XLA Modules:
  0.0 34.9 jit_solution(2134483242225016414)
XLA Ops:
  0.6 32.9 %shard_map.93 = (f32[1024,128]{1,0:T(8,128)S(1)}, f32[1024,128]{1,0:T(8,128)S(1)}, f32[1024,128]{1,0:T(8,128)S(1)}, f32[1024,128]{1,0:T(8,128)S(1)}) custom-call(f32[1024,128]{1,0:T(8,128)} %bitcast.10, f32[1024,128]{1,0:T(8,128)} %bitcast.11, f32[1024,128]{1,0:T(8,128)} %bitcast.12, f32[1024,128]{1,0:T(8,128)} %bitcast.13, f32[1024,128]{1,0:T(8,128)} %bitcast.14, ...), custom_call_target="tpu_custom_call" | custom-call | tf_op jit(solution)/shard_map/pallas_call | solution.py:442
  33.5 1.3 %shard_map.94 = (f32[1024,128]{1,0:T(8,128)}, f32[1024,128]{1,0:T(8,128)}, f32[1024,128]{1,0:T(8,128)}, f32[1024,128]{1,0:T(8,128)}) custom-call(f32[1024,128]{1,0:T(8,128)S(1)} %get-tuple-element.12.u, f32[1024,128]{1,0:T(8,128)S(1)} %get-tuple-element.13.v, f32[1024,128]{1,0:T(8,128)S(1)} %get-tuple-element.14.w, f32[1024,128]{1,0:T(8,128)S(1)} %get-tuple-element.15.p), custom_call_target="tpu_custom_call" | custom-call | tf_op jit(solution)/shard_map/pallas_call | solution.py:470

commit v3 on v2

--- a/solution.py
+++ b/solution.py
@@ -18,8 +18,8 @@
 def kernel(
     K, nx, ny, nz,
     u_in, v_in, w_in, p_in, b_in, s_in,
-    uo, vo, w, p,
-    us, vs, s, bi, bj, E, D, H, X, Y, ps, h,
+    uo, vo, w, ps, X, Y, s, ends,
+    p, us, vs, bi, bj, E, D, H, h,
     i_low, i_high, i_from_up, i_from_down,
     j_own, j_to_right, j_to_left, j_from_left, j_from_right,
     hu, hbi, hv, hbj, C, vbr,
@@ -200,7 +200,7 @@
         return x, y
 
     x, y = each(responses, ((one, one), (zero, zero)))
-    for n, val in enumerate((x, y, Z, B)):
+    for n, val in enumerate((x, y, B)):
         for m in range(2):
             cmine[16 * n + 8 * m:16 * n + 8 * m + 8, :] = val[m]
             cgath[me, 16 * n + 8 * m:16 * n + 8 * m + 8, :] = val[m]
@@ -337,22 +337,22 @@
             betas = [None] * nz
             for d in range(nz - 1, -1, -1):
                 R = 1.0 / (1.0 - crow(d, 1) * beta)
-                zbr = crow(d, 2) * beta * R
-                lam = crow(d, 2) + zbr * crow(d, 1)
+                zbr = crow(d, 0) * beta * R
+                lam = crow(d, 0) + zbr * crow(d, 1)
                 red[d, 0:16, :] = lam
                 for name, val in (("beta", beta), ("r", R), ("aw", zbr), ("lam", lam)):
                     pick(name, d, val)
-                beta = crow(d, 3) + zbr * crow(d, 0)
+                beta = crow(d, 2) + zbr * crow(d, 0)
                 betas[d] = beta
             psi = nothing
             for d in range(nz):
-                xr = crow(d, 0) / (1.0 - psi * crow(d, 3))
+                xr = crow(d, 0) / (1.0 - psi * crow(d, 2))
                 xrp = xr * psi
                 red[d, 16:32, :] = xr
                 pick("psi", d, psi)
                 pick("r2", d, 1.0 / (1.0 - psi * betas[d]))
                 pick("wa", d, xrp)
-                psi = crow(d, 1) + xrp * crow(d, 2)
+                psi = crow(d, 1) + xrp * crow(d, 0)
             for n, name in enumerate(picks):
                 mine[16 * n:16 * n + 16, :] = picks[name]
 
@@ -391,6 +391,9 @@
             alpha = jnp.where(me < d, fgath[t, d] + red[d, 0:16, :] * alpha, alpha)
         wb = r2 * (omega + psi * (down_row + lam * alpha))
         pa = alpha + beta * (r * (W0 + crow(me, 1) * alpha + crow(me, 0) * wb))
+        if final:
+            ends[0:16, :], ends[16:32, :] = wb, pa
+            break
         wb2, pa2 = (wb[0:8], wb[8:16]), (pa[0:8], pa[8:16])
 
         def implicit(g, wprev):
@@ -402,28 +405,41 @@
                 pn = tuple(star[m] - ss[m] * (wn[m] - wprev[m]) for m in range(2))
                 put_pair(w, g, j, wn)
                 put_pair(p, g, j, pn)
-                if not final:
-                    acc = pack_edges(g, j, pn, acc, i_low.at[t + 1], i_high.at[t + 1], 0)
+                acc = pack_edges(g, j, pn, acc, i_low.at[t + 1], i_high.at[t + 1], 0)
                 wprev = wn
-            if not final:
-                j_own[t + 1, pl.ds(pl.multiple_of(g * 8, 8), 8), :] = acc
+            j_own[t + 1, pl.ds(pl.multiple_of(g * 8, 8), 8), :] = acc
             return wprev
 
         each(implicit, wb2)
-        if not final:
-            dense(t + 1, False)
-            halos = halo_copies(t + 1)
-            for c in halos:
-                c.start()
-
-
-def store(u, v, w, p, u_out, v_out, w_out, p_out, sem):
+        dense(t + 1, False)
+        halos = halo_copies(t + 1)
+        for c in halos:
+            c.start()
+
+
+def store(u, v, w, ps, X, Y, s, ends, u_out, v_out, w_out, p_out, wo, po, sem):
+    rows = w.shape[0] // 4
     copies = [
         pltpu.make_async_copy(src, dst, sem.at[n])
-        for n, (src, dst) in enumerate(((u, u_out), (v, v_out), (w, w_out), (p, p_out)))
+        for n, (src, dst) in enumerate(((u, u_out), (v, v_out)))
     ]
     for c in copies:
         c.start()
+    wb, pa = ends[0:16, :], ends[16:32, :]
+    wprev = wb
+    for part in range(4):
+        for l in range(part * rows, (part + 1) * rows, 16):
+            wn = w[l:l + 16, :] + X[l:l + 16, :] * wb + Y[l:l + 16, :] * pa
+            wo[l:l + 16, :] = wn
+            po[l:l + 16, :] = ps[l:l + 16, :] - s[l:l + 16, :] * (wn - wprev)
+            wprev = wn
+        for n, (src, dst) in enumerate(((wo, w_out), (po, p_out))):
+            c = pltpu.make_async_copy(
+                src.at[pl.ds(part * rows, rows)], dst.at[pl.ds(part * rows, rows)],
+                sem.at[2 + 2 * part + n],
+            )
+            c.start()
+            copies.append(c)
     for c in copies:
         c.wait()
 
@@ -441,18 +457,18 @@
         jdense = pltpu.VMEM((T, KJ, J), F32)
         outs = pl.pallas_call(
             functools.partial(kernel, K, nx, ny, nz),
-            out_shape=[full] * 4,
+            out_shape=[full] * 7 + [pltpu.VMEM((32, J), F32)],
             in_specs=[pl.BlockSpec(memory_space=pl.ANY)] * 6,
-            out_specs=[pl.BlockSpec(memory_space=pltpu.VMEM)] * 4,
-            scratch_shapes=[full] * 12 + [ihalo] * 4 + [jhalo] + [jdense] * 4 + [
+            out_specs=[pl.BlockSpec(memory_space=pltpu.VMEM)] * 8,
+            scratch_shapes=[full] * 9 + [ihalo] * 4 + [jhalo] + [jdense] * 4 + [
                 pltpu.VMEM((2 * K + 16, J), F32),
                 pltpu.VMEM((2 * K + 16, J), F32),
                 pltpu.VMEM((KJ, J), F32),
                 pltpu.VMEM((KJ, J), F32),
                 pltpu.VMEM((KJ, J), F32),
                 pltpu.VMEM((KJ, J), F32),
-                pltpu.VMEM((64, J), F32),
-                pltpu.VMEM((nz, 64, J), F32),
+                pltpu.VMEM((48, J), F32),
+                pltpu.VMEM((nz, 48, J), F32),
                 pltpu.VMEM((T, 2, 16, J), F32),
                 pltpu.VMEM((T, nz, 16, J), F32),
                 pltpu.VMEM((nz, 32, J), F32),
@@ -465,14 +481,17 @@
                 pltpu.SemaphoreType.DMA((T, max(nz - 1, 1))),
                 pltpu.SemaphoreType.DMA((T, max(nz - 1, 1))),
             ],
-            compiler_params=pltpu.CompilerParams(collective_id=0, has_side_effects=True),
+            compiler_params=pltpu.CompilerParams(
+                collective_id=0, has_side_effects=True, vmem_limit_bytes=61800 * 1024
+            ),
         )(*(f.reshape(R, J) for f in fields))
         outs = pl.pallas_call(
             store,
             out_shape=[jax.ShapeDtypeStruct((R, J), F32)] * 4,
-            in_specs=[pl.BlockSpec(memory_space=pltpu.VMEM)] * 4,
+            in_specs=[pl.BlockSpec(memory_space=pltpu.VMEM)] * 8,
             out_specs=[pl.BlockSpec(memory_space=pl.ANY)] * 4,
-            scratch_shapes=[pltpu.SemaphoreType.DMA((4,))],
+            scratch_shapes=[full, full, pltpu.SemaphoreType.DMA((10,))],
+            compiler_params=pltpu.CompilerParams(vmem_limit_bytes=61800 * 1024),
         )(*(pltpu.with_memory_space_constraint(o, pltpu.VMEM) for o in outs))
         return tuple(o.reshape(K, I, J) for o in outs)
 

time: 35 us -> 35.1 us (level)
  no operation moved by 1% of the time
where the time goes in v3:
time: 35.1 us; the launch traced here: 35 us
  Pallas kernels  34.3 us (98%)
  between operations  0.64 us (2%)
    pallas_call x1, Pallas kernels, shards(): pl.pallas_call(functools.partial(kernel, K, nx, ny, nz), out_shape=[full]...  32.9 us
    pallas_call x1, Pallas kernels, shards(): pl.pallas_call(store, out_shape=[jax.ShapeDtypeStruct((R, J), F32)] * 4,...  1.39 us

profile of v3, /device:TPU:0, one launch (start us, length us, event | category | flops | bytes accessed | tf_op | source)
XLA Modules:
  0.0 35.0 jit_solution(9349774138214196255)
XLA Ops:
  0.6 32.9 %shard_map.93 = (f32[1024,128]{1,0:T(8,128)S(1)}, f32[1024,128]{1,0:T(8,128)S(1)}, f32[1024,128]{1,0:T(8,128)S(1)}, f32[1024,128]{1,0:T(8,128)S(1)}, f32[1024,12...) custom-call(f32[1024,128]{1,0:T(8,128)} %bitcast.10, ...), custom_call_target="tpu_custom_call" | custom-call | tf_op jit(solution)/shard_map/pallas_call | solution.py:458
  33.6 1.4 %shard_map.94 = (f32[1024,128]{1,0:T(8,128)}, f32[1024,128]{1,0:T(8,128)}, f32[1024,128]{1,0:T(8,128)}, f32[1024,128]{1,0:T(8,128)}) custom-call(f32[1024,128]{1,0:T(8,128)S(1)} %get-tuple-element.16.u, f32[1024,128]{1,0:T(8,128)S(1)} %get-tuple-element.17.v, f32[1024,128]{1,0:T(8,128)S(1)} %get-tuple-element.18.w, f32[1024,128]{1,0:T(8,128)S(1)} %get-tuple-element.19.ps, ...), custom_call_target="tpu_custom_call" | custom-call | tf_op jit(solution)/shard_map/pallas_call | solution.py:488
